TPU v7x, 32 devices: a whole 2x2x4 slice. The times are simulated.
32 devices in a mesh: rows: 2 (over core), cols: 4 (over z), slabs: 4 (over y, x).
Axes of the slice: x: 2, y: 2, z: 4, core: 2. Of those that a mesh axis runs over, the one named last changes fastest.
Arguments:
- density: float32 [32, 384, 32, 128], P('rows', 'cols', 'slabs'), may hold values from 0.5 to 2
- flow_j: float32 [32, 384, 32, 128], P('rows', 'cols', 'slabs'), may hold values from -0.3 to 0.3
- flow_i: float32 [32, 384, 32, 128], P('rows', 'cols', 'slabs'), may hold values from -0.3 to 0.3
- flow_k: float32 [32, 384, 32, 128], P('rows', 'cols', 'slabs'), may hold values from -0.3 to 0.3
Outputs:
- anomaly: float32 [32, 384, 32, 128], P('rows', 'cols', 'slabs')
- density_end: float32 [32, 384, 32, 128], P('rows', 'cols', 'slabs')
All inputs are finite; a program needn't handle non-finite values.
Results may differ from a plain program's by a relative error of at most 0.00002.
Values sent between devices are 32-bit elements; how exact they have to be, the bound alone decides.
A program may use at most 128 MiB of HBM per device.

v0:
```python
import jax
import jax.numpy as jnp
from jax import lax
from jax.sharding import PartitionSpec as P

STEPS = 6


def with_halo(block, sides, width):
    for axis, dim in sides:
        count = lax.axis_size(axis)
        forward = [(i, i + 1) for i in range(count - 1)]
        backward = [(target, source) for source, target in forward]
        low = lax.ppermute(
            lax.slice_in_dim(block, block.shape[dim] - width, None, axis=dim), axis, forward
        )
        high = lax.ppermute(lax.slice_in_dim(block, 0, width, axis=dim), axis, backward)
        block = jnp.concatenate([low, block, high], axis=dim)
    return block


def inner_cells(values, dims):
    for dim in dims:
        values = lax.slice_in_dim(values, 1, values.shape[dim] - 1, axis=dim)
    return values


def side_cells(values, dim, start, dims):
    others = [other for other in dims if other != dim]
    values = inner_cells(values, others)
    return lax.slice_in_dim(values, start, start + values.shape[dim] - 2, axis=dim)


def advance(padded, flow_j, flow_i, flow_k):
    middle = inner_cells(padded, (0, 1, 2))
    lower = [side_cells(padded, dim, 0, (0, 1, 2)) for dim in (0, 1, 2)]
    upper = [side_cells(padded, dim, 2, (0, 1, 2)) for dim in (0, 1, 2)]
    slopes = [above - below for above, below in zip(upper, lower)]
    smooth_rate = 0.05
    spread = lower[0] + upper[0] + lower[1] + upper[1] + lower[2] + upper[2] - 6.0 * middle
    return (
        middle - flow_j * slopes[0] - flow_i * slopes[1] - flow_k * slopes[2] + smooth_rate * spread
    )


def body(density, flow_j, flow_i, flow_k):
    for step in range(STEPS):
        padded = with_halo(density, (("rows", 0), ("cols", 1), ("slabs", 2)), 1)
        density = advance(padded, flow_j, flow_i, flow_k)
    count = density.shape[2] * lax.axis_size("slabs")
    guess = 1.0
    moved = density - guess
    totals, squares = lax.psum(
        (jnp.sum(moved, axis=2, keepdims=True), jnp.sum(moved * moved, axis=2, keepdims=True)),
        "slabs",
    )
    line_mean = guess + totals / count
    centred = density - line_mean
    line_variance = squares / count - totals / count * (totals / count)
    anomaly = centred * lax.rsqrt(line_variance + 0.0001)
    return (anomaly, density)


def solution(mesh):
    placed = (
        P("rows", "cols", "slabs", None),
        P("rows", "cols", "slabs", None),
        P("rows", "cols", "slabs", None),
        P("rows", "cols", "slabs", None),
    )
    return jax.shard_map(
        body,
        mesh=mesh,
        in_specs=placed,
        out_specs=(P("rows", "cols", "slabs", None), P("rows", "cols", "slabs", None)),
        check_vma=False,
    )
```

profile of v0, /device:TPU:0, one launch (start us, length us, event | category | flops | bytes accessed | tf_op | source)
XLA Modules:
  0.0 600.9 jit_solution(7399973700371125411)
XLA Ops:
  8.4 2.4 collective-permute-start.1
  12.9 3.3 constant_dynamic-update-slice_fusion.1
  16.3 4.3 collective-permute-start.3
  20.6 1.6 collective-permute-start.2
  23.1 4.8 collective-permute-done.2
  30.8 4.6 collective-permute-start.5
  35.4 20.0 %collective-permute-done.4 = f32[18,98,1,128]{3,1,2,0:T(8,128)S(1)} collective-permute-done((f32[18,98,1,128]{3,1,2,0:T(8,128)S(1)}, f32[18,98,1,128]{3,1,2,0:T(8,128)S(1)}, u32[]{:S(2)}, u32[]{:S(2)}) %collective-permute-start.4) | collective-permute-done | bytes 903200 | tf_op jit(solution)/shard_map/ppermute | solution.py:17
  57.3 23.0 %multiply_add_fusion.5 = f32[16,96,8,128]{3,2,1,0:T(8,128)} fusion(f32[16,96,8,128]{3,2,1,0:T(8,128)} %param.4, f32[16,96,8,128]{3,2,1,0:T(8,128)S(1)} %bitcast.7, f32[18,98,1,128]{3,2,1,0:T(1,128)S(1)} %copy.34, f32[18,1,8,128]{3,2,1,0:T(8,128)S(1)} %collective-permute-done.2, f32[18,96,8,128]{3,2,1,0:T(8,128)} %copy-done.5, ...), kind=kLoop, calls=%fused_computation.107 | loop fusion | flops 44040192 | bytes 41275392 | tf_op jit(solution)/shard_map/add | solution.py:42
  84.4 2.3 collective-permute-done.6
  87.6 3.5 collective-permute-start.9
  93.0 4.6 collective-permute-done.8
  97.6 2.2 pad_maximum_fusion.120
  101.2 21.2 %collective-permute-start.11 = (f32[18,98,1,128]{3,1,2,0:T(8,128)S(1)}, f32[18,98,1,128]{3,1,2,0:T(8,128)S(1)}, u32[]{:S(2)}, u32[]{:S(2)}) collective-permute-start(f32[18,98,1,128]{3,1,2,0:T(8,128)S(1)} %copy.39), channel_id=1, source_target_pairs={{0,1},{1,2},{2,3},{4,5},{5,6},{6,7},{8,9},{9,10},{10,11},{12,13},{... | collective-permute-start | bytes 2709512 | tf_op jit(solution)/shard_map/ppermute | solution.py:14
  122.4 19.7 %collective-permute-done.10 = f32[18,98,1,128]{3,1,2,0:T(8,128)S(1)} collective-permute-done((f32[18,98,1,128]{3,1,2,0:T(8,128)S(1)}, f32[18,98,1,128]{3,1,2,0:T(8,128)S(1)}, u32[]{:S(2)}, u32[]{:S(2)}) %collective-permute-start.10) | collective-permute-done | bytes 903200 | tf_op jit(solution)/shard_map/ppermute | solution.py:17
  144.0 22.8 %multiply_add_fusion.4 = f32[16,96,8,128]{3,2,1,0:T(8,128)} fusion(f32[16,96,8,128]{3,2,1,0:T(8,128)} %multiply_add_fusion.5, f32[16,96,8,128]{3,2,1,0:T(8,128)S(1)} %bitcast.7, f32[18,98,1,128]{3,2,1,0:T(1,128)S(1)} %copy.38, f32[18,1,8,128]{3,2,1,0:T(8,128)S(1)} %collective-permute-done.8, f32[1,96,8,128]{3,2,1,0:T(8,128)S(1)} %collective-permute-done.6, ...), kind=kLoop, calls=%fused_computation.106 | loop fusion | flops 56623104 | bytes 34197504 | tf_op jit(solution)/shard_map/add | solution.py:42
  170.9 2.3 collective-permute-done.12
  174.1 3.3 collective-permute-start.15
  179.4 4.3 collective-permute-done.14
  183.7 2.2 pad_maximum_fusion.115
  187.3 19.7 %collective-permute-start.17 = (f32[18,98,1,128]{3,1,2,0:T(8,128)S(1)}, f32[18,98,1,128]{3,1,2,0:T(8,128)S(1)}, u32[]{:S(2)}, u32[]{:S(2)}) collective-permute-start(f32[18,98,1,128]{3,1,2,0:T(8,128)S(1)} %copy.43), channel_id=1, source_target_pairs={{0,1},{1,2},{2,3},{4,5},{5,6},{6,7},{8,9},{9,10},{10,11},{12,13},{... | collective-permute-start | bytes 2709512 | tf_op jit(solution)/shard_map/ppermute | solution.py:14
  207.1 20.0 %collective-permute-done.16 = f32[18,98,1,128]{3,1,2,0:T(8,128)S(1)} collective-permute-done((f32[18,98,1,128]{3,1,2,0:T(8,128)S(1)}, f32[18,98,1,128]{3,1,2,0:T(8,128)S(1)}, u32[]{:S(2)}, u32[]{:S(2)}) %collective-permute-start.16) | collective-permute-done | bytes 903200 | tf_op jit(solution)/shard_map/ppermute | solution.py:17
  229.0 21.9 %multiply_add_fusion.3 = f32[16,96,8,128]{3,2,1,0:T(8,128)} fusion(f32[16,96,8,128]{3,2,1,0:T(8,128)} %multiply_add_fusion.4, f32[16,96,8,128]{3,2,1,0:T(8,128)S(1)} %bitcast.7, f32[18,98,1,128]{3,2,1,0:T(1,128)S(1)} %copy.42, f32[18,1,8,128]{3,2,1,0:T(8,128)S(1)} %collective-permute-done.14, f32[1,96,8,128]{3,2,1,0:T(8,128)S(1)} %collective-permute-done.12, ...), kind=kLoop, calls=%fused_computation.105 | loop fusion | flops 56623104 | bytes 34197504 | tf_op jit(solution)/shard_map/add | solution.py:42
  255.0 2.3 collective-permute-done.18
  258.2 2.2 collective-permute-start.21
  260.4 1.8 collective-permute-start.20
  262.3 4.3 collective-permute-done.20
  266.6 2.2 pad_maximum_fusion.110
  270.2 19.7 %collective-permute-start.23 = (f32[18,98,1,128]{3,1,2,0:T(8,128)S(1)}, f32[18,98,1,128]{3,1,2,0:T(8,128)S(1)}, u32[]{:S(2)}, u32[]{:S(2)}) collective-permute-start(f32[18,98,1,128]{3,1,2,0:T(8,128)S(1)} %copy.47), channel_id=1, source_target_pairs={{0,1},{1,2},{2,3},{4,5},{5,6},{6,7},{8,9},{9,10},{10,11},{12,13},{... | collective-permute-start | bytes 2709512 | tf_op jit(solution)/shard_map/ppermute | solution.py:14
  290.0 20.0 %collective-permute-done.22 = f32[18,98,1,128]{3,1,2,0:T(8,128)S(1)} collective-permute-done((f32[18,98,1,128]{3,1,2,0:T(8,128)S(1)}, f32[18,98,1,128]{3,1,2,0:T(8,128)S(1)}, u32[]{:S(2)}, u32[]{:S(2)}) %collective-permute-start.22) | collective-permute-done | bytes 903200 | tf_op jit(solution)/shard_map/ppermute | solution.py:17
  311.9 22.8 %multiply_add_fusion.2 = f32[16,96,8,128]{3,2,1,0:T(8,128)} fusion(f32[16,96,8,128]{3,2,1,0:T(8,128)} %multiply_add_fusion.3, f32[16,96,8,128]{3,2,1,0:T(8,128)S(1)} %bitcast.7, f32[18,98,1,128]{3,2,1,0:T(1,128)S(1)} %copy.46, f32[18,1,8,128]{3,2,1,0:T(8,128)S(1)} %collective-permute-done.20, f32[1,96,8,128]{3,2,1,0:T(8,128)S(1)} %collective-permute-done.18, ...), kind=kLoop, calls=%fused_computation.104 | loop fusion | flops 56623104 | bytes 34197504 | tf_op jit(solution)/shard_map/add | solution.py:42
  338.8 2.3 collective-permute-done.24
  342.0 2.2 collective-permute-start.27
  346.2 4.3 collective-permute-done.26
  350.4 2.2 pad_maximum_fusion.105
  354.1 19.9 %collective-permute-start.29 = (f32[18,98,1,128]{3,1,2,0:T(8,128)S(1)}, f32[18,98,1,128]{3,1,2,0:T(8,128)S(1)}, u32[]{:S(2)}, u32[]{:S(2)}) collective-permute-start(f32[18,98,1,128]{3,1,2,0:T(8,128)S(1)} %copy.51), channel_id=1, source_target_pairs={{0,1},{1,2},{2,3},{4,5},{5,6},{6,7},{8,9},{9,10},{10,11},{12,13},{... | collective-permute-start | bytes 2709512 | tf_op jit(solution)/shard_map/ppermute | solution.py:14
  374.0 19.8 %collective-permute-done.28 = f32[18,98,1,128]{3,1,2,0:T(8,128)S(1)} collective-permute-done((f32[18,98,1,128]{3,1,2,0:T(8,128)S(1)}, f32[18,98,1,128]{3,1,2,0:T(8,128)S(1)}, u32[]{:S(2)}, u32[]{:S(2)}) %collective-permute-start.28) | collective-permute-done | bytes 903200 | tf_op jit(solution)/shard_map/ppermute | solution.py:17
  395.7 21.9 %multiply_add_fusion.1 = f32[16,96,8,128]{3,2,1,0:T(8,128)} fusion(f32[16,96,8,128]{3,2,1,0:T(8,128)} %multiply_add_fusion.2, f32[16,96,8,128]{3,2,1,0:T(8,128)S(1)} %bitcast.7, f32[18,98,1,128]{3,2,1,0:T(1,128)S(1)} %copy.50, f32[18,1,8,128]{3,2,1,0:T(8,128)S(1)} %collective-permute-done.26, f32[1,96,8,128]{3,2,1,0:T(8,128)S(1)} %collective-permute-done.24, ...), kind=kLoop, calls=%fused_computation.103 | loop fusion | flops 56623104 | bytes 34197504 | tf_op jit(solution)/shard_map/add | solution.py:42
  421.7 2.3 collective-permute-done.30
  425.0 2.2 collective-permute-start.33
  429.2 4.3 collective-permute-done.32
  433.5 2.2 pad_maximum_fusion.104
  435.7 19.1 %collective-permute-start.35 = (f32[18,98,1,128]{3,1,2,0:T(8,128)S(1)}, f32[18,98,1,128]{3,1,2,0:T(8,128)S(1)}, u32[]{:S(2)}, u32[]{:S(2)}) collective-permute-start(f32[18,98,1,128]{3,1,2,0:T(8,128)S(1)} %copy.55), channel_id=1, source_target_pairs={{0,1},{1,2},{2,3},{4,5},{5,6},{6,7},{8,9},{9,10},{10,11},{12,13},{... | collective-permute-start | bytes 2709512 | tf_op jit(solution)/shard_map/ppermute | solution.py:14
  456.4 17.7 %collective-permute-done.35 = f32[18,98,1,128]{3,1,2,0:T(8,128)S(1)} collective-permute-done((f32[18,98,1,128]{3,1,2,0:T(8,128)S(1)}, f32[18,98,1,128]{3,1,2,0:T(8,128)S(1)}, u32[]{:S(2)}, u32[]{:S(2)}) %collective-permute-start.35) | collective-permute-done | bytes 903200 | tf_op jit(solution)/shard_map/ppermute | solution.py:14
  475.1 23.4 %collective-permute-done.34 = f32[18,98,1,128]{3,1,2,0:T(8,128)S(1)} collective-permute-done((f32[18,98,1,128]{3,1,2,0:T(8,128)S(1)}, f32[18,98,1,128]{3,1,2,0:T(8,128)S(1)}, u32[]{:S(2)}, u32[]{:S(2)}) %collective-permute-start.34) | collective-permute-done | bytes 903200 | tf_op jit(solution)/shard_map/ppermute | solution.py:17
  499.4 28.4 %add_reduce_fusion = (f32[16,96,128]{2,1,0:T(8,128)}, f32[16,96,128]{2,1,0:T(8,128)}, f32[16,96,8,128]{3,2,1,0:T(8,128)}) fusion(f32[16,96,8,128]{3,2,1,0:T(8,128)} %multiply_add_fusion.1, f32[16,96,8,128]{3,2,1,0:T(8,128)S(1)} %bitcast.7, f32[18,1,8,128]{3,2,1,0:T(8,128)S(1)} %collective-permute-done.32, f32[1,96,8,128]{3,2,1,0:T(8,128)} %copy-done.7, ...), kind=kLoop, calls=%fused_computation.108 | loop fusion | flops 62521344 | bytes 35770368 | tf_op jit(solution)/shard_map/reduce_sum | solution.py:54
  527.8 59.2 %all-reduce.3.cloned.1.call-done = (f32[16,96,1,128]{3,1,0,2:T(8,128)}, f32[16,96,1,128]{3,1,0,2:T(8,128)}) async-done(((f32[16,96,1,128]{3,1,0,2:T(8,128)}, f32[16,96,1,128]{3,1,0,2:T(8,128)}), (f32[16,96,1,128]{3,1,0,2:T(8,128)}, f32[16,96,1,128]{3,1,0,2:T(8,128)})) %all-reduce.3.cloned.1.call-update) | async-done | bytes 1572880 | tf_op jit(solution)/shard_map/psum | solution.py:53
  587.0 1.6 add_bitcast_fusion
  588.6 5.2 subtract_multiply_fusion
  (110 shorter events, 58.4 us)
Async XLA Ops:
  7.2 579.8 %all-reduce.3.cloned.1.call-start = ((), (), s32[]{:S(2)}) async-start(), calls=%async_computation | async-start | bytes 3145728 | tf_op jit(solution)/shard_map/psum | solution.py:53
  8.4 3.7 collective-permute-start.1
  10.8 5.4 collective-permute-start
  16.2 14.6 %copy-start.9 = (f32[1,96,8,128]{3,2,1,0:T(8,128)}, f32[1,96,8,128]{3,2,1,0:T(8,128)S(1)}, u32[]{:S(2)}) copy-start(f32[1,96,8,128]{3,2,1,0:T(8,128)S(1)} %collective-permute-done) | copy-start | bytes 1179652
  16.3 14.5 %copy-start.5 = (f32[18,96,8,128]{3,2,1,0:T(8,128)}, f32[18,96,8,128]{3,2,1,0:T(8,128)S(1)}, u32[]{:S(2)}) copy-start(f32[18,96,8,128]{3,2,1,0:T(8,128)S(1)} %constant_dynamic-update-slice_fusion) | copy-start | bytes 21233668
  16.3 6.8 %collective-permute-start.3 = (f32[18,1,8,128]{3,2,1,0:T(8,128)S(1)}, f32[18,1,8,128]{3,2,1,0:T(8,128)S(1)}, u32[]{:S(2)}, u32[]{:S(2)}) collective-permute-start(f32[18,1,8,128]{3,2,1,0:T(8,128)S(1)} %get-tuple-element.31), channel_id=1, source_target_pairs={{0,4},{4,8},{8,12},{1,5},{5,9},{9,13},{2,6},{6,10},{10,14},{3,7},{... | collective-permute-start | bytes 221192 | tf_op jit(solution)/shard_map/ppermute | solution.py:14
  20.6 36.7 %slice-start = ((s8[6291456]{0:T(1024)(128)(4,1)}), s8[4194304]{0:T(1024)(128)(4,1)S(1)}, s32[]{:S(2)}) async-start(s8[6291456]{0:T(1024)(128)(4,1)} %bitcast.6), calls=%async_computation.1 | async-start | bytes 8388608
  20.6 36.7 %slice-start.1 = ((s8[6291456]{0:T(1024)(128)(4,1)}), s8[2097152]{0:T(1024)(128)(4,1)S(1)}, s32[]{:S(2)}) async-start(s8[6291456]{0:T(1024)(128)(4,1)} %bitcast.6), calls=%async_computation.2 | async-start | bytes 4194304
  20.6 7.3 %collective-permute-start.2 = (f32[18,1,8,128]{3,2,1,0:T(8,128)S(1)}, f32[18,1,8,128]{3,2,1,0:T(8,128)S(1)}, u32[]{:S(2)}, u32[]{:S(2)}) collective-permute-start(f32[18,1,8,128]{3,2,1,0:T(8,128)S(1)} %get-tuple-element.32), channel_id=1, source_target_pairs={{4,0},{8,4},{12,8},{5,1},{9,5},{13,9},{6,2},{10,6},{14,10},{7,3},{... | collective-permute-start | bytes 221192 | tf_op jit(solution)/shard_map/ppermute | solution.py:17
  29.4 26.0 %collective-permute-start.4 = (f32[18,98,1,128]{3,1,2,0:T(8,128)S(1)}, f32[18,98,1,128]{3,1,2,0:T(8,128)S(1)}, u32[]{:S(2)}, u32[]{:S(2)}) collective-permute-start(f32[18,98,1,128]{3,1,2,0:T(8,128)S(1)} %copy.33), channel_id=1, source_target_pairs={{1,0},{2,1},{3,2},{5,4},{6,5},{7,6},{9,8},{10,9},{11,10},{13,12},{... | collective-permute-start | bytes 2709512 | tf_op jit(solution)/shard_map/ppermute | solution.py:17
  30.8 25.5 %collective-permute-start.5 = (f32[18,98,1,128]{3,1,2,0:T(8,128)S(1)}, f32[18,98,1,128]{3,1,2,0:T(8,128)S(1)}, u32[]{:S(2)}, u32[]{:S(2)}) collective-permute-start(f32[18,98,1,128]{3,1,2,0:T(8,128)S(1)} %copy.35), channel_id=1, source_target_pairs={{0,1},{1,2},{2,3},{4,5},{5,6},{6,7},{8,9},{9,10},{10,11},{12,13},{... | collective-permute-start | bytes 2709512 | tf_op jit(solution)/shard_map/ppermute | solution.py:14
  80.3 17.3 %copy-start.4 = (f32[16,96,8,128]{3,2,1,0:T(8,128)S(1)}, f32[16,96,8,128]{3,2,1,0:T(8,128)}, u32[]{:S(2)}) copy-start(f32[16,96,8,128]{3,2,1,0:T(8,128)} %multiply_add_fusion.5) | copy-start | bytes 18874372
  81.6 2.8 collective-permute-start.7
  83.1 3.6 collective-permute-start.6
  87.6 5.5 collective-permute-start.9
  91.1 52.9 %slice-start.2 = ((s8[6291456]{0:T(1024)(128)(4,1)}), s8[4194304]{0:T(1024)(128)(4,1)S(1)}, s32[]{:S(2)}) async-start(s8[6291456]{0:T(1024)(128)(4,1)} %bitcast.8), calls=%async_computation.3 | async-start | bytes 8388608
  91.1 52.9 %slice-start.3 = ((s8[6291456]{0:T(1024)(128)(4,1)}), s8[2097152]{0:T(1024)(128)(4,1)S(1)}, s32[]{:S(2)}) async-start(s8[6291456]{0:T(1024)(128)(4,1)} %bitcast.8), calls=%async_computation.4 | async-start | bytes 4194304
  91.1 6.5 %collective-permute-start.8 = (f32[18,1,8,128]{3,2,1,0:T(8,128)S(1)}, f32[18,1,8,128]{3,2,1,0:T(8,128)S(1)}, u32[]{:S(2)}, u32[]{:S(2)}) collective-permute-start(f32[18,1,8,128]{3,2,1,0:T(8,128)S(1)} %get-tuple-element.30), channel_id=1, source_target_pairs={{4,0},{8,4},{12,8},{5,1},{9,5},{13,9},{6,2},{10,6},{14,10},{7,3},{... | collective-permute-start | bytes 221192 | tf_op jit(solution)/shard_map/ppermute | solution.py:17
  99.8 42.3 %collective-permute-start.10 = (f32[18,98,1,128]{3,1,2,0:T(8,128)S(1)}, f32[18,98,1,128]{3,1,2,0:T(8,128)S(1)}, u32[]{:S(2)}, u32[]{:S(2)}) collective-permute-start(f32[18,98,1,128]{3,1,2,0:T(8,128)S(1)} %copy.37), channel_id=1, source_target_pairs={{1,0},{2,1},{3,2},{5,4},{6,5},{7,6},{9,8},{10,9},{11,10},{13,12},{... | collective-permute-start | bytes 2709512 | tf_op jit(solution)/shard_map/ppermute | solution.py:17
  101.2 41.8 %collective-permute-start.11 = (f32[18,98,1,128]{3,1,2,0:T(8,128)S(1)}, f32[18,98,1,128]{3,1,2,0:T(8,128)S(1)}, u32[]{:S(2)}, u32[]{:S(2)}) collective-permute-start(f32[18,98,1,128]{3,1,2,0:T(8,128)S(1)} %copy.39), channel_id=1, source_target_pairs={{0,1},{1,2},{2,3},{4,5},{5,6},{6,7},{8,9},{9,10},{10,11},{12,13},{... | collective-permute-start | bytes 2709512 | tf_op jit(solution)/shard_map/ppermute | solution.py:14
  166.8 16.8 %copy-start.1 = (f32[16,96,8,128]{3,2,1,0:T(8,128)S(1)}, f32[16,96,8,128]{3,2,1,0:T(8,128)}, u32[]{:S(2)}) copy-start(f32[16,96,8,128]{3,2,1,0:T(8,128)} %multiply_add_fusion.4) | copy-start | bytes 18874372
  168.2 2.8 collective-permute-start.13
  169.6 3.6 collective-permute-start.12
  174.1 5.3 collective-permute-start.15
  177.4 6.2 %collective-permute-start.14 = (f32[18,1,8,128]{3,2,1,0:T(8,128)S(1)}, f32[18,1,8,128]{3,2,1,0:T(8,128)S(1)}, u32[]{:S(2)}, u32[]{:S(2)}) collective-permute-start(f32[18,1,8,128]{3,2,1,0:T(8,128)S(1)} %get-tuple-element.28), channel_id=1, source_target_pairs={{4,0},{8,4},{12,8},{5,1},{9,5},{13,9},{6,2},{10,6},{14,10},{7,3},{... | collective-permute-start | bytes 221192 | tf_op jit(solution)/shard_map/ppermute | solution.py:17
  185.9 41.1 %collective-permute-start.16 = (f32[18,98,1,128]{3,1,2,0:T(8,128)S(1)}, f32[18,98,1,128]{3,1,2,0:T(8,128)S(1)}, u32[]{:S(2)}, u32[]{:S(2)}) collective-permute-start(f32[18,98,1,128]{3,1,2,0:T(8,128)S(1)} %copy.41), channel_id=1, source_target_pairs={{1,0},{2,1},{3,2},{5,4},{6,5},{7,6},{9,8},{10,9},{11,10},{13,12},{... | collective-permute-start | bytes 2709512 | tf_op jit(solution)/shard_map/ppermute | solution.py:17
  187.3 40.7 %collective-permute-start.17 = (f32[18,98,1,128]{3,1,2,0:T(8,128)S(1)}, f32[18,98,1,128]{3,1,2,0:T(8,128)S(1)}, u32[]{:S(2)}, u32[]{:S(2)}) collective-permute-start(f32[18,98,1,128]{3,1,2,0:T(8,128)S(1)} %copy.43), channel_id=1, source_target_pairs={{0,1},{1,2},{2,3},{4,5},{5,6},{6,7},{8,9},{9,10},{10,11},{12,13},{... | collective-permute-start | bytes 2709512 | tf_op jit(solution)/shard_map/ppermute | solution.py:14
  250.9 15.7 %copy-start.2 = (f32[16,96,8,128]{3,2,1,0:T(8,128)S(1)}, f32[16,96,8,128]{3,2,1,0:T(8,128)}, u32[]{:S(2)}) copy-start(f32[16,96,8,128]{3,2,1,0:T(8,128)} %multiply_add_fusion.3) | copy-start | bytes 18874372
  252.2 2.8 collective-permute-start.19
  253.6 3.6 collective-permute-start.18
  258.2 4.2 collective-permute-start.21
  260.4 6.2 %collective-permute-start.20 = (f32[18,1,8,128]{3,2,1,0:T(8,128)S(1)}, f32[18,1,8,128]{3,2,1,0:T(8,128)S(1)}, u32[]{:S(2)}, u32[]{:S(2)}) collective-permute-start(f32[18,1,8,128]{3,2,1,0:T(8,128)S(1)} %get-tuple-element.26), channel_id=1, source_target_pairs={{4,0},{8,4},{12,8},{5,1},{9,5},{13,9},{6,2},{10,6},{14,10},{7,3},{... | collective-permute-start | bytes 221192 | tf_op jit(solution)/shard_map/ppermute | solution.py:17
  268.9 41.1 %collective-permute-start.22 = (f32[18,98,1,128]{3,1,2,0:T(8,128)S(1)}, f32[18,98,1,128]{3,1,2,0:T(8,128)S(1)}, u32[]{:S(2)}, u32[]{:S(2)}) collective-permute-start(f32[18,98,1,128]{3,1,2,0:T(8,128)S(1)} %copy.45), channel_id=1, source_target_pairs={{1,0},{2,1},{3,2},{5,4},{6,5},{7,6},{9,8},{10,9},{11,10},{13,12},{... | collective-permute-start | bytes 2709512 | tf_op jit(solution)/shard_map/ppermute | solution.py:17
  270.2 40.7 %collective-permute-start.23 = (f32[18,98,1,128]{3,1,2,0:T(8,128)S(1)}, f32[18,98,1,128]{3,1,2,0:T(8,128)S(1)}, u32[]{:S(2)}, u32[]{:S(2)}) collective-permute-start(f32[18,98,1,128]{3,1,2,0:T(8,128)S(1)} %copy.47), channel_id=1, source_target_pairs={{0,1},{1,2},{2,3},{4,5},{5,6},{6,7},{8,9},{9,10},{10,11},{12,13},{... | collective-permute-start | bytes 2709512 | tf_op jit(solution)/shard_map/ppermute | solution.py:14
  334.7 15.7 %copy-start.3 = (f32[16,96,8,128]{3,2,1,0:T(8,128)S(1)}, f32[16,96,8,128]{3,2,1,0:T(8,128)}, u32[]{:S(2)}) copy-start(f32[16,96,8,128]{3,2,1,0:T(8,128)} %multiply_add_fusion.2) | copy-start | bytes 18874372
  336.0 2.8 collective-permute-start.25
  337.5 3.6 collective-permute-start.24
  342.0 4.2 collective-permute-start.27
  344.2 6.2 %collective-permute-start.26 = (f32[18,1,8,128]{3,2,1,0:T(8,128)S(1)}, f32[18,1,8,128]{3,2,1,0:T(8,128)S(1)}, u32[]{:S(2)}, u32[]{:S(2)}) collective-permute-start(f32[18,1,8,128]{3,2,1,0:T(8,128)S(1)} %get-tuple-element.24), channel_id=1, source_target_pairs={{4,0},{8,4},{12,8},{5,1},{9,5},{13,9},{6,2},{10,6},{14,10},{7,3},{... | collective-permute-start | bytes 221192 | tf_op jit(solution)/shard_map/ppermute | solution.py:17
  352.7 41.1 %collective-permute-start.28 = (f32[18,98,1,128]{3,1,2,0:T(8,128)S(1)}, f32[18,98,1,128]{3,1,2,0:T(8,128)S(1)}, u32[]{:S(2)}, u32[]{:S(2)}) collective-permute-start(f32[18,98,1,128]{3,1,2,0:T(8,128)S(1)} %copy.49), channel_id=1, source_target_pairs={{1,0},{2,1},{3,2},{5,4},{6,5},{7,6},{9,8},{10,9},{11,10},{13,12},{... | collective-permute-start | bytes 2709512 | tf_op jit(solution)/shard_map/ppermute | solution.py:17
  354.1 40.7 %collective-permute-start.29 = (f32[18,98,1,128]{3,1,2,0:T(8,128)S(1)}, f32[18,98,1,128]{3,1,2,0:T(8,128)S(1)}, u32[]{:S(2)}, u32[]{:S(2)}) collective-permute-start(f32[18,98,1,128]{3,1,2,0:T(8,128)S(1)} %copy.51), channel_id=1, source_target_pairs={{0,1},{1,2},{2,3},{4,5},{5,6},{6,7},{8,9},{9,10},{10,11},{12,13},{... | collective-permute-start | bytes 2709512 | tf_op jit(solution)/shard_map/ppermute | solution.py:14
  417.6 15.9 %copy-start = (f32[16,96,8,128]{3,2,1,0:T(8,128)S(1)}, f32[16,96,8,128]{3,2,1,0:T(8,128)}, u32[]{:S(2)}) copy-start(f32[16,96,8,128]{3,2,1,0:T(8,128)} %multiply_add_fusion.1) | copy-start | bytes 18874372
  418.9 2.8 collective-permute-start.31
  420.4 3.6 collective-permute-start.30
  425.0 4.2 collective-permute-start.33
  427.2 6.2 %collective-permute-start.32 = (f32[18,1,8,128]{3,2,1,0:T(8,128)S(1)}, f32[18,1,8,128]{3,2,1,0:T(8,128)S(1)}, u32[]{:S(2)}, u32[]{:S(2)}) collective-permute-start(f32[18,1,8,128]{3,2,1,0:T(8,128)S(1)} %get-tuple-element.22), channel_id=1, source_target_pairs={{4,0},{8,4},{12,8},{5,1},{9,5},{13,9},{6,2},{10,6},{14,10},{7,3},{... | collective-permute-start | bytes 221192 | tf_op jit(solution)/shard_map/ppermute | solution.py:17
  435.7 38.4 %collective-permute-start.35 = (f32[18,98,1,128]{3,1,2,0:T(8,128)S(1)}, f32[18,98,1,128]{3,1,2,0:T(8,128)S(1)}, u32[]{:S(2)}, u32[]{:S(2)}) collective-permute-start(f32[18,98,1,128]{3,1,2,0:T(8,128)S(1)} %copy.55), channel_id=1, source_target_pairs={{0,1},{1,2},{2,3},{4,5},{5,6},{6,7},{8,9},{9,10},{10,11},{12,13},{... | collective-permute-start | bytes 2709512 | tf_op jit(solution)/shard_map/ppermute | solution.py:14
  454.9 43.6 %collective-permute-start.34 = (f32[18,98,1,128]{3,1,2,0:T(8,128)S(1)}, f32[18,98,1,128]{3,1,2,0:T(8,128)S(1)}, u32[]{:S(2)}, u32[]{:S(2)}) collective-permute-start(f32[18,98,1,128]{3,1,2,0:T(8,128)S(1)} %copy.53), channel_id=1, source_target_pairs={{1,0},{2,1},{3,2},{5,4},{6,5},{7,6},{9,8},{10,9},{11,10},{13,12},{... | collective-permute-start | bytes 2709512 | tf_op jit(solution)/shard_map/ppermute | solution.py:17
  (3 other events, 26.4 us)
Sparse Core Ops, SparseCore 0:
  528.0 58.9 all-reduce.2
where the time goes:
time: 608 us; the launch traced here: 601 us
  waiting for transfers between devices  241 us (40%)
  other arithmetic  164 us (27%)
  starting transfers between devices  156 us (26%)
  local copies, waits for them, and re-layouts  23.8 us (4%)
  between operations  15 us (2%)
    ppermute x18, waiting for transfers between devices, with_halo(): lax.ppermute(lax.slice_in_dim(block, 0, width, axis=dim), axis, backward)  161 us
    ppermute x18, starting transfers between devices, with_halo(): lax.ppermute(lax.slice_in_dim(block, block.shape[dim] - width, None, axis...  132 us
    add x5, other arithmetic, advance(): middle - flow_j * slopes[0] - flow_i * slopes[1] - flow_k * slopes[2]  112 us
    psum x1, waiting for transfers between devices, body(): lax.psum((jnp.sum(moved, axis=2, keepdims=True), jnp.sum(moved * moved, a...  59.2 us
    reduce_sum x1, other arithmetic, body(): jnp.sum(moved, axis=2, keepdims=True)  28.4 us
    ppermute x18, starting transfers between devices, with_halo(): lax.ppermute(lax.slice_in_dim(block, 0, width, axis=dim), axis, backward)  24.5 us
    ppermute x18, waiting for transfers between devices, with_halo(): lax.ppermute(lax.slice_in_dim(block, block.shape[dim] - width, None, axis...  21.1 us
    concatenate x10, other arithmetic, with_halo(): block = jnp.concatenate([low, block, high], axis=dim)  14.7 us
  transfers between devices with their start and end apart: 37, of which 25 were waited for; matrix products, arithmetic and copies ran while one was open for 2% of the time, Pallas kernels for 0%

commit v1 on v0

v1 whole, which is shorter than its diff:
```python
import functools

import jax
import jax.numpy as jnp
from jax import lax
from jax.experimental import pallas as pl
from jax.experimental.pallas import tpu as pltpu
from jax.sharding import PartitionSpec as P

STEPS = 6
CHUNK = 2
MESH = pl.DeviceIdType.MESH


def advance_kernel(
    sizes, dens, flow_j, flow_i, flow_k, out,
    st, fl, hk, sk, in_sem, fl_sem, out_sem,
    k_send, k_recv, i_send, i_recv, j_send, j_recv,
):
    n_r, n_c, n_s = sizes
    n_j, n_i, n_k, n_l = dens.shape
    chunks = n_j // CHUNK
    r, q, s = lax.axis_index("rows"), lax.axis_index("cols"), lax.axis_index("slabs")
    places = {"rows": (r, n_r), "cols": (q, n_c), "slabs": (s, n_s)}

    def sends(axis, d):
        at, count = places[axis]
        return at < count - 1 if d == 0 else at > 0

    def takes(axis, d):
        at, count = places[axis]
        return at > 0 if d == 0 else at < count - 1

    def beside(axis, d):
        at, count = places[axis]
        return {axis: jnp.minimum(at + 1, count - 1) if d == 0 else jnp.maximum(at - 1, 0)}

    def remote(src, dst, send, recv, axis, d):
        return pltpu.make_async_remote_copy(
            src_ref=src, dst_ref=dst, send_sem=send, recv_sem=recv,
            device_id=beside(axis, d), device_id_type=MESH,
        )

    def k_copy(slot, c, d):
        rows = pl.ds(c * CHUNK, CHUNK)
        return remote(
            sk.at[slot, d, rows], hk.at[slot, d, rows],
            k_send.at[slot, d, c], k_recv.at[slot, d, c], "slabs", d,
        )

    def i_copy(slot, c, d):
        rows = pl.ds(c * CHUNK + 1, CHUNK)
        src, dst = (n_i, 0) if d == 0 else (1, n_i + 1)
        return remote(
            st.at[slot, rows, src], st.at[slot, rows, dst],
            i_send.at[slot, d, c], i_recv.at[slot, d, c], "cols", d,
        )

    def j_copy(slot, d):
        src, dst = (n_j, 0) if d == 0 else (1, n_j + 1)
        cells = pl.ds(1, n_i)
        return remote(
            st.at[slot, src, cells], st.at[slot, dst, cells],
            j_send.at[slot, d], j_recv.at[slot, d], "rows", d,
        )

    def last_of(c, d):
        return c == (chunks - 1 if d == 0 else 0)

    def first_of(c, d):
        return c == (0 if d == 0 else chunks - 1)

    def start_sends(slot, c):
        for d in (0, 1):
            @pl.when(jnp.logical_and(sends("rows", d), last_of(c, d)))
            def _():
                j_copy(slot, d).start()

            @pl.when(sends("cols", d))
            def _():
                i_copy(slot, c, d).start()

            @pl.when(sends("slabs", d))
            def _():
                k_copy(slot, c, d).start()

    def wait_sends(slot, c):
        for d in (0, 1):
            @pl.when(jnp.logical_and(sends("rows", d), last_of(c, d)))
            def _():
                j_copy(slot, d).wait_send()

            @pl.when(sends("cols", d))
            def _():
                i_copy(slot, c, d).wait_send()

            @pl.when(sends("slabs", d))
            def _():
                k_copy(slot, c, d).wait_send()

    def wait_halos(slot, c):
        for d in (0, 1):
            @pl.when(jnp.logical_and(takes("rows", d), first_of(c, d)))
            def _():
                j_copy(slot, d).wait_recv()

            @pl.when(takes("cols", d))
            def _():
                i_copy(slot, c, d).wait_recv()

            @pl.when(takes("slabs", d))
            def _():
                k_copy(slot, c, d).wait_recv()

    def dens_copy(c):
        return pltpu.make_async_copy(
            dens.at[pl.ds(c * CHUNK, CHUNK)],
            st.at[0, pl.ds(c * CHUNK + 1, CHUNK), pl.ds(1, n_i)],
            in_sem.at[c],
        )

    def flow_copy(c, d):
        rows = pl.ds(c * CHUNK, CHUNK)
        return pltpu.make_async_copy(
            (flow_j, flow_i, flow_k)[d].at[rows], fl.at[d, rows], fl_sem.at[d, c]
        )

    def out_copy(c):
        return pltpu.make_async_copy(
            st.at[STEPS % 2, pl.ds(c * CHUNK + 1, CHUNK), pl.ds(1, n_i)],
            out.at[pl.ds(c * CHUNK, CHUNK)],
            out_sem.at[c],
        )

    def order(p):
        return jnp.where(lax.rem(r, 2) == 0, chunks - 1 - p, p)

    def load(p, carry):
        dens_copy(order(p)).start()
        return carry

    def load_flows(p, carry):
        for d in range(3):
            flow_copy(order(p), d).start()
        return carry

    lax.fori_loop(0, chunks, load, 0)
    lax.fori_loop(0, chunks, load_flows, 0)

    for d in (0, 1):
        @pl.when(jnp.logical_not(takes("slabs", d)))
        def _():
            def clear(j, carry):
                for slot in (0, 1):
                    hk[slot, d, j] = jnp.zeros((n_i, n_l), jnp.float32)
                return carry

            lax.fori_loop(0, n_j, clear, 0)

        @pl.when(jnp.logical_not(takes("cols", d)))
        def _():
            for slot in (0, 1):
                for j in range(n_j):
                    st[slot, j + 1, 0 if d == 0 else n_i + 1] = jnp.zeros((n_k, n_l), jnp.float32)

        @pl.when(jnp.logical_not(takes("rows", d)))
        def _():
            def clear(i, carry):
                for slot in (0, 1):
                    st[slot, 0 if d == 0 else n_j + 1, i + 1] = jnp.zeros((n_k, n_l), jnp.float32)
                return carry

            lax.fori_loop(0, n_i, clear, 0)

    barrier = pltpu.get_barrier_semaphore()
    for axis in ("rows", "cols", "slabs"):
        for d in (0, 1):
            @pl.when(sends(axis, d))
            def _():
                pl.semaphore_signal(barrier, inc=1, device_id=beside(axis, d), device_id_type=MESH)
    pl.semaphore_wait(
        barrier,
        sum(takes(axis, d).astype(jnp.int32) for axis in ("rows", "cols", "slabs") for d in (0, 1)),
    )

    group = 8 if n_i % 8 == 0 else 1

    def keep_faces(slot, j, i, value):
        sk[slot, 0, j, pl.ds(i, 1)] = value[n_k - 1:n_k]
        sk[slot, 1, j, pl.ds(i, 1)] = value[0:1]

    def first_faces(p, carry):
        c = order(p)
        dens_copy(c).wait()
        for jj in range(CHUNK):
            j = c * CHUNK + jj

            def cells(g, carry):
                i0 = pl.multiple_of(g * group, group)
                for e in range(group):
                    keep_faces(0, j, i0 + e, st[0, j + 1, i0 + e + 1])
                return carry

            lax.fori_loop(0, n_i // group, cells, 0)
        start_sends(0, c)
        return carry

    lax.fori_loop(0, chunks, first_faces, 0)

    level = lax.broadcasted_iota(jnp.int32, (n_k, n_l), 0)
    bottom, top = level == 0, level == n_k - 1

    def advance(now, later, c):
        for jj in range(CHUNK):
            j = c * CHUNK + jj

            def cells(g, carry):
                i0 = pl.multiple_of(g * group, group)
                line = [st[now, j + 1, i0 + e] for e in range(group + 2)]
                for e in range(group):
                    i = i0 + e
                    middle = line[e + 1]
                    low_i, high_i = line[e], line[e + 2]
                    low_j, high_j = st[now, j, i + 1], st[now, j + 2, i + 1]
                    low_k = jnp.where(bottom, hk[now, 0, j, pl.ds(i, 1)], pltpu.roll(middle, 1, 0))
                    high_k = jnp.where(
                        top, hk[now, 1, j, pl.ds(i, 1)], pltpu.roll(middle, n_k - 1, 0)
                    )
                    spread = low_j + high_j + low_i + high_i + low_k + high_k - 6.0 * middle
                    value = (
                        middle
                        - fl[0, j, i] * (high_j - low_j)
                        - fl[1, j, i] * (high_i - low_i)
                        - fl[2, j, i] * (high_k - low_k)
                        + 0.05 * spread
                    )
                    st[later, j + 1, i + 1] = value
                    keep_faces(later, j, i, value)
                return carry

            lax.fori_loop(0, n_i // group, cells, 0)

    def step(p, carry):
        t, c = p // chunks, order(lax.rem(p, chunks))
        now = lax.rem(t, 2)
        later = 1 - now

        @pl.when(t == 0)
        def _():
            for d in range(3):
                flow_copy(c, d).wait()

        wait_halos(now, c)

        @pl.when(t > 0)
        def _():
            wait_sends(later, c)

        advance(now, later, c)

        @pl.when(t < STEPS - 1)
        def _():
            start_sends(later, c)

        @pl.when(t == STEPS - 1)
        def _():
            out_copy(c).start()

        return carry

    lax.fori_loop(0, STEPS * chunks, step, 0)

    def finish(c, carry):
        wait_sends((STEPS - 1) % 2, c)
        out_copy(c).wait()
        return carry

    lax.fori_loop(0, chunks, finish, 0)


def body(sizes, density, flow_j, flow_i, flow_k):
    n_j, n_i, n_k, n_l = density.shape
    chunks = n_j // CHUNK
    dma = pltpu.SemaphoreType.DMA
    density = pl.pallas_call(
        functools.partial(advance_kernel, sizes),
        out_shape=jax.ShapeDtypeStruct(density.shape, density.dtype),
        in_specs=[pl.BlockSpec(memory_space=pl.ANY)] * 4,
        out_specs=pl.BlockSpec(memory_space=pl.ANY),
        scratch_shapes=[
            pltpu.VMEM((2, n_j + 2, n_i + 2, n_k, n_l), jnp.float32),
            pltpu.VMEM((3, n_j, n_i, n_k, n_l), jnp.float32),
            pltpu.VMEM((2, 2, n_j, n_i, n_l), jnp.float32),
            pltpu.VMEM((2, 2, n_j, n_i, n_l), jnp.float32),
            dma((chunks,)), dma((3, chunks)), dma((chunks,)),
            dma((2, 2, chunks)), dma((2, 2, chunks)),
            dma((2, 2, chunks)), dma((2, 2, chunks)),
            dma((2, 2)), dma((2, 2)),
        ],
        compiler_params=pltpu.CompilerParams(
            collective_id=0, has_side_effects=True, vmem_limit_bytes=60 * 1024 * 1024
        ),
    )(density, flow_j, flow_i, flow_k)
    count = density.shape[2] * lax.axis_size("slabs")
    guess = 1.0
    moved = density - guess
    totals, squares = lax.psum(
        (jnp.sum(moved, axis=2, keepdims=True), jnp.sum(moved * moved, axis=2, keepdims=True)),
        "slabs",
    )
    line_mean = guess + totals / count
    centred = density - line_mean
    line_variance = squares / count - totals / count * (totals / count)
    anomaly = centred * lax.rsqrt(line_variance + 0.0001)
    return (anomaly, density)


def solution(mesh):
    sizes = tuple(mesh.shape[axis] for axis in ("rows", "cols", "slabs"))
    spec = P("rows", "cols", "slabs", None)
    return jax.shard_map(
        functools.partial(body, sizes),
        mesh=mesh,
        in_specs=(spec,) * 4,
        out_specs=(spec,) * 2,
        check_vma=False,
    )
```

time: 608 us -> 306 us (0.50); the launches traced: 601 us -> 306 us
  Pallas kernels: 0 us -> 213 us
  waiting for transfers between devices: 241 us -> 61.3 us
  starting transfers between devices: 156 us -> 0.04 us
  other arithmetic: 164 us -> 15.5 us
  local copies, waits for them, and re-layouts: 23.8 us -> 2.71 us
    pallas_call x0 -> x1, Pallas kernels: none -> 213 us  [body(): pl.pallas_call(functools.partial(advance_kernel, sizes), out_shape=jax.Sh...]
    ppermute x36 -> x0, waiting for transfers between devices: 182 us -> none  [the longest x18 161 us: with_halo(): lax.ppermute(lax.slice_in_dim(block, 0, width, axis=dim), axis, backward)]
    ppermute x36 -> x0, starting transfers between devices: 156 us -> none  [the longest x18 132 us: with_halo(): lax.ppermute(lax.slice_in_dim(block, block.shape[dim] - width, None, axis...]
    add x5 -> x0, other arithmetic: 112 us -> none  [advance(): middle - flow_j * slopes[0] - flow_i * slopes[1] - flow_k * slopes[2]]
    reduce_sum x1, other arithmetic: 28.4 us -> 8.08 us  [body(): jnp.sum(moved, axis=2, keepdims=True)]
    concatenate x10 -> x0, other arithmetic: 14.7 us -> none  [with_halo(): block = jnp.concatenate([low, block, high], axis=dim)]
    ppermute x12 -> x0, local copies, waits for them, and re-layouts: 11.2 us -> none  [the longest x6 5.58 us: with_halo(): lax.ppermute(lax.slice_in_dim(block, block.shape[dim] - width, None, axis...]
    slice x19 -> x0, local copies, waits for them, and re-layouts: 8.53 us -> none  [the longest x12 6.98 us: with_halo(): lax.slice_in_dim(block, block.shape[dim] - width, None, axis=dim)]
  transfers between devices with their start and end apart: 37 -> 1, of which waited for: 25 -> 1; matrix products, arithmetic and copies ran while one was open for 2% -> 0% of each run, Pallas kernels for 0% -> 0%
where the time goes in v1:
time: 306 us
  Pallas kernels  213 us (70%)
  waiting for transfers between devices  61.3 us (20%)
  other arithmetic  15.5 us (5%)
  between operations  14.1 us (5%)
    pallas_call x1, Pallas kernels, body(): pl.pallas_call(functools.partial(advance_kernel, sizes), out_shape=jax.Sh...  213 us
    psum x1, waiting for transfers between devices, body(): lax.psum((jnp.sum(moved, axis=2, keepdims=True), jnp.sum(moved * moved, a...  61.3 us
    reduce_sum x1, other arithmetic, body(): jnp.sum(moved, axis=2, keepdims=True)  8.08 us
  transfers between devices with their start and end apart: 1, of which 1 were waited for; matrix products, arithmetic and copies ran while one was open for 0% of the time, Pallas kernels for 0%

profile of v1, /device:TPU:0, one launch (start us, length us, event | category | flops | bytes accessed | tf_op | source)
XLA Modules:
  0.0 306.3 jit_solution(15915661755165909559)
XLA Ops:
  7.2 0.0 all-reduce.3.cloned.1.call-start
  7.2 212.8 %shard_map.59 = f32[16,96,8,128]{3,2,1,0:T(8,128)} custom-call(f32[16,96,8,128]{3,2,1,0:T(8,128)} %dens.1, f32[16,96,8,128]{3,2,1,0:T(8,128)} %flow_j.1, f32[16,96,8,128]{3,2,1,0:T(8,128)} %flow_i.1, f32[16,96,8,128]{3,2,1,0:T(8,128)} %flow_k.1), custom_call_target="tpu_custom_call" | custom-call | tf_op jit(solution)/shard_map/pallas_call | solution.py:285
  220.0 8.1 %add_reduce_fusion = (f32[16,96,128]{2,1,0:T(8,128)}, f32[16,96,128]{2,1,0:T(8,128)}) fusion(f32[16,96,8,128]{3,2,1,0:T(8,128)} %shard_map.59), kind=kLoop, calls=%fused_computation.2 | loop fusion | flops 5898240 | bytes 7864320 | tf_op jit(solution)/shard_map/reduce_sum | solution.py:308
  228.1 0.0 all-reduce.3.cloned.1.call-update
  228.1 61.3 %all-reduce.3.cloned.1.call-done = (f32[16,96,1,128]{3,1,0,2:T(8,128)}, f32[16,96,1,128]{3,1,0,2:T(8,128)}) async-done(((f32[16,96,1,128]{3,1,0,2:T(8,128)}, f32[16,96,1,128]{3,1,0,2:T(8,128)}), (f32[16,96,1,128]{3,1,0,2:T(8,128)}, f32[16,96,1,128]{3,1,0,2:T(8,128)})) %all-reduce.3.cloned.1.call-update) | async-done | bytes 1572880 | tf_op jit(solution)/shard_map/psum | solution.py:307
  289.3 0.0 slice-start
  289.3 1.7 add_bitcast_fusion
  291.1 0.0 slice-start.1
  291.1 5.7 %subtract_multiply_fusion = f32[16,96,8,128]{3,2,1,0:T(8,128)} fusion(f32[16,96,8,128]{3,2,1,0:T(8,128)} %shard_map.59, f32[16,96,128]{2,1,0:T(8,128)S(1)} %get-tuple-element.7, f32[16,96,128]{2,1,0:T(8,128)S(1)} %get-tuple-element.6), kind=kLoop, calls=%fused_computation.1 | loop fusion | flops 3145728 | bytes 14155776 | tf_op jit(solution)/shard_map/mul | solution.py:314
  296.8 0.0 slice-done
  296.8 0.0 slice-done.1
  296.8 2.7 copy.9
  (1 shorter events, 0.0 us)
Async XLA Ops:
  7.2 282.2 %all-reduce.3.cloned.1.call-start = ((), (), s32[]{:S(2)}) async-start(), calls=%async_computation | async-start | bytes 3145728 | tf_op jit(solution)/shard_map/psum | solution.py:307
  289.3 7.4 %slice-start = ((s8[6291456]{0:T(1024)(128)(4,1)}), s8[4194304]{0:T(1024)(128)(4,1)S(1)}, s32[]{:S(2)}) async-start(s8[6291456]{0:T(1024)(128)(4,1)} %bitcast.6), calls=%async_computation.1 | async-start | bytes 8388608
  291.1 5.7 %slice-start.1 = ((s8[6291456]{0:T(1024)(128)(4,1)}), s8[2097152]{0:T(1024)(128)(4,1)S(1)}, s32[]{:S(2)}) async-start(s8[6291456]{0:T(1024)(128)(4,1)} %bitcast.6), calls=%async_computation.2 | async-start | bytes 4194304
Sparse Core Ops, SparseCore 0:
  228.2 61.0 all-reduce.2

commit v2 on v1

--- a/solution.py
+++ b/solution.py
@@ -276,6 +276,28 @@
         return carry
 
     lax.fori_loop(0, chunks, finish, 0)
+
+
+def line_sums(totals, squares):
+    if lax.axis_size("slabs") != 4 or totals.shape[1] % 2:
+        return lax.psum((totals, squares), "slabs")
+    s = lax.axis_index("slabs")
+
+    def swap(values, bit):
+        return lax.ppermute(values, "slabs", [(i, i ^ bit) for i in range(4)])
+
+    half = totals.shape[1] // 2
+    found = []
+    for start, first, second in ((0, 1, 2), (half, 2, 1)):
+        total, square = (
+            lax.slice_in_dim(values, start, start + half, axis=1) for values in (totals, squares)
+        )
+        low = (s // first) % 2 == 0
+        part = jnp.where(low, total, square) + swap(jnp.where(low, square, total), first)
+        part = part + swap(part, second)
+        other = swap(part, first)
+        found.append((jnp.where(low, part, other), jnp.where(low, other, part)))
+    return [jnp.concatenate(pair, axis=1) for pair in zip(*found)]
 
 
 def body(sizes, density, flow_j, flow_i, flow_k):
@@ -304,9 +326,8 @@
     count = density.shape[2] * lax.axis_size("slabs")
     guess = 1.0
     moved = density - guess
-    totals, squares = lax.psum(
-        (jnp.sum(moved, axis=2, keepdims=True), jnp.sum(moved * moved, axis=2, keepdims=True)),
-        "slabs",
+    totals, squares = line_sums(
+        jnp.sum(moved, axis=2, keepdims=True), jnp.sum(moved * moved, axis=2, keepdims=True)
     )
     line_mean = guess + totals / count
     centred = density - line_mean

time: 306 us -> 274 us (0.90)
  waiting for transfers between devices: 61.3 us -> 34.6 us
  between operations: 14.1 us -> 0.74 us
  starting transfers between devices: 0.04 us -> 6.99 us
    psum x1 -> x0, waiting for transfers between devices: 61.3 us -> none  [body(): lax.psum((jnp.sum(moved, axis=2, keepdims=True), jnp.sum(moved * moved, a...]
    ppermute x0 -> x6, waiting for transfers between devices: none -> 34.6 us  [swap(): return lax.ppermute(values, 'slabs', [(i, i ^ bit) for i in range(4)])]
    ppermute x0 -> x6, starting transfers between devices: none -> 6.99 us  [swap(): return lax.ppermute(values, 'slabs', [(i, i ^ bit) for i in range(4)])]
  transfers between devices with their start and end apart: 1 -> 6, of which waited for: 1 -> 6; matrix products, arithmetic and copies ran while one was open for 0% -> 0% of each run, Pallas kernels for 0% -> 0%
where the time goes in v2:
time: 274 us
  Pallas kernels  213 us (78%)
  waiting for transfers between devices  34.6 us (13%)
  other arithmetic  15.8 us (6%)
  starting transfers between devices  6.99 us (3%)
    pallas_call x1, Pallas kernels, body(): pl.pallas_call(functools.partial(advance_kernel, sizes), out_shape=jax.Sh...  213 us
    ppermute x6, waiting for transfers between devices, swap(): return lax.ppermute(values, 'slabs', [(i, i ^ bit) for i in range(4)])  34.6 us
    reduce_sum x1, other arithmetic, body(): jnp.sum(moved, axis=2, keepdims=True)  7.95 us
    ppermute x6, starting transfers between devices, swap(): return lax.ppermute(values, 'slabs', [(i, i ^ bit) for i in range(4)])  6.99 us
  transfers between devices with their start and end apart: 6, of which 6 were waited for; matrix products, arithmetic and copies ran while one was open for 0% of the time, Pallas kernels for 0%

profile of v2, /device:TPU:0, one launch (start us, length us, event | category | flops | bytes accessed | tf_op | source)
XLA Modules:
  0.0 273.5 jit_solution(15115021954451398563)
XLA Ops:
  0.6 212.7 %shard_map.59 = f32[16,96,8,128]{3,2,1,0:T(8,128)} custom-call(f32[16,96,8,128]{3,2,1,0:T(8,128)} %dens.1, f32[16,96,8,128]{3,2,1,0:T(8,128)} %flow_j.1, f32[16,96,8,128]{3,2,1,0:T(8,128)} %flow_i.1, f32[16,96,8,128]{3,2,1,0:T(8,128)} %flow_k.1), custom_call_target="tpu_custom_call" | custom-call | tf_op jit(solution)/shard_map/pallas_call | solution.py:307
  213.4 0.0 slice-start
  213.4 7.9 %add_reduce_fusion = (f32[16,96,128]{2,1,0:T(8,128)S(1)}, f32[16,96,128]{2,1,0:T(8,128)}) fusion(f32[16,96,8,128]{3,2,1,0:T(8,128)} %shard_map.59), kind=kLoop, calls=%fused_computation.2 | loop fusion | flops 5898240 | bytes 7864320 | tf_op jit(solution)/shard_map/reduce_sum | solution.py:330
  221.4 1.8 slice_select_fusion.1
  223.1 1.6 collective-permute-start
  224.7 0.0 slice-start.1
  224.7 8.3 %collective-permute-done = f32[16,48,1,128]{3,1,0,2:T(8,128)S(1)} collective-permute-done((f32[16,48,1,128]{3,1,0,2:T(8,128)}, f32[16,48,1,128]{3,1,0,2:T(8,128)S(1)}, u32[]{:S(2)}, u32[]{:S(2)}) %collective-permute-start) | collective-permute-done | bytes 393248 | tf_op jit(solution)/shard_map/ppermute | solution.py:287
  233.0 1.2 select_add_fusion.1
  234.2 0.1 collective-permute-start.3
  234.3 2.0 collective-permute-start.1
  236.3 10.0 %collective-permute-done.3 = f32[16,48,1,128]{3,1,0,2:T(8,128)S(1)} collective-permute-done((f32[16,48,1,128]{3,1,0,2:T(8,128)S(1)}, f32[16,48,1,128]{3,1,0,2:T(8,128)S(1)}, u32[]{:S(2)}, u32[]{:S(2)}) %collective-permute-start.3) | collective-permute-done | bytes 393248 | tf_op jit(solution)/shard_map/ppermute | solution.py:287
  246.3 1.1 select_add_fusion
  247.4 1.6 collective-permute-start.4
  249.0 2.5 collective-permute-done.1
  251.5 0.1 add.46
  251.5 1.7 collective-permute-start.2
  253.2 6.1 %collective-permute-done.4 = f32[16,48,1,128]{3,1,0,2:T(8,128)S(1)} collective-permute-done((f32[16,48,1,128]{3,1,0,2:T(8,128)S(1)}, f32[16,48,1,128]{3,1,0,2:T(8,128)S(1)}, u32[]{:S(2)}, u32[]{:S(2)}) %collective-permute-start.4) | collective-permute-done | bytes 393248 | tf_op jit(solution)/shard_map/ppermute | solution.py:287
  259.3 0.1 collective-permute-start.5
  259.4 4.2 %collective-permute-done.2 = f32[16,48,1,128]{3,1,0,2:T(8,128)S(1)} collective-permute-done((f32[16,48,1,128]{3,1,0,2:T(8,128)S(1)}, f32[16,48,1,128]{3,1,0,2:T(8,128)S(1)}, u32[]{:S(2)}, u32[]{:S(2)}) %collective-permute-start.2) | collective-permute-done | bytes 393248 | tf_op jit(solution)/shard_map/ppermute | solution.py:287
  263.6 0.1 select_bitcast_fusion.3
  263.7 3.5 %collective-permute-done.5 = f32[16,48,1,128]{3,1,0,2:T(8,128)S(1)} collective-permute-done((f32[16,48,1,128]{3,1,0,2:T(8,128)S(1)}, f32[16,48,1,128]{3,1,0,2:T(8,128)S(1)}, u32[]{:S(2)}, u32[]{:S(2)}) %collective-permute-start.5) | collective-permute-done | bytes 393248 | tf_op jit(solution)/shard_map/ppermute | solution.py:287
  267.2 0.1 select_bitcast_fusion.2
  267.2 0.2 fusion.3
  267.5 0.0 slice-done
  267.5 0.0 slice-done.1
  267.5 3.3 %subtract_multiply_fusion = f32[16,96,8,128]{3,2,1,0:T(8,128)} fusion(f32[16,96,8,128]{3,2,1,0:T(8,128)S(1)} %bitcast.11, f32[16,96,128]{2,1,0:T(8,128)S(1)} %get-tuple-element.7, f32[16,96,128]{2,1,0:T(8,128)S(1)} %get-tuple-element.6), kind=kLoop, calls=%fused_computation | loop fusion | flops 3145728 | bytes 14155776 | tf_op jit(solution)/shard_map/mul | solution.py:335
  270.8 2.7 copy.7
  (2 shorter events, 0.0 us)
Async XLA Ops:
  213.4 54.1 %slice-start = ((s8[6291456]{0:T(1024)(128)(4,1)}), s8[2097152]{0:T(1024)(128)(4,1)S(1)}, s32[]{:S(2)}) async-start(s8[6291456]{0:T(1024)(128)(4,1)} %bitcast.10), calls=%async_computation | async-start | bytes 4194304
  223.1 9.8 %collective-permute-start = (f32[16,48,1,128]{3,1,0,2:T(8,128)}, f32[16,48,1,128]{3,1,0,2:T(8,128)S(1)}, u32[]{:S(2)}, u32[]{:S(2)}) collective-permute-start(f32[16,48,1,128]{3,1,0,2:T(8,128)} %slice_select_fusion.1), channel_id=1, source_target_pairs={{0,1},{1,0},{2,3},{3,2},{4,5},{5,4},{6,7},{7,6},{8,9},{9,8},{10,11... | collective-permute-start | bytes 1179656 | tf_op jit(solution)/shard_map/ppermute | solution.py:287
  224.7 42.8 %slice-start.1 = ((s8[6291456]{0:T(1024)(128)(4,1)}), s8[4194304]{0:T(1024)(128)(4,1)S(1)}, s32[]{:S(2)}) async-start(s8[6291456]{0:T(1024)(128)(4,1)} %bitcast.10), calls=%async_computation.1 | async-start | bytes 8388608
  234.2 12.1 %collective-permute-start.3 = (f32[16,48,1,128]{3,1,0,2:T(8,128)S(1)}, f32[16,48,1,128]{3,1,0,2:T(8,128)S(1)}, u32[]{:S(2)}, u32[]{:S(2)}) collective-permute-start(f32[16,48,1,128]{3,1,0,2:T(8,128)S(1)} %get-tuple-element.5), channel_id=1, source_target_pairs={{0,2},{1,3},{2,0},{3,1},{4,6},{5,7},{6,4},{7,5},{8,10},{9,11},{10,... | collective-permute-start | bytes 1179656 | tf_op jit(solution)/shard_map/ppermute | solution.py:287
  234.3 17.2 %collective-permute-start.1 = (f32[16,48,1,128]{3,1,0,2:T(8,128)S(1)}, f32[16,48,1,128]{3,1,0,2:T(8,128)S(1)}, u32[]{:S(2)}, u32[]{:S(2)}) collective-permute-start(f32[16,48,1,128]{3,1,0,2:T(8,128)S(1)} %get-tuple-element.4), channel_id=1, source_target_pairs={{0,2},{1,3},{2,0},{3,1},{4,6},{5,7},{6,4},{7,5},{8,10},{9,11},{10,... | collective-permute-start | bytes 1179656 | tf_op jit(solution)/shard_map/ppermute | solution.py:287
  247.4 11.9 %collective-permute-start.4 = (f32[16,48,1,128]{3,1,0,2:T(8,128)S(1)}, f32[16,48,1,128]{3,1,0,2:T(8,128)S(1)}, u32[]{:S(2)}, u32[]{:S(2)}) collective-permute-start(f32[16,48,1,128]{3,1,0,2:T(8,128)S(1)} %select_add_fusion), channel_id=1, source_target_pairs={{0,1},{1,0},{2,3},{3,2},{4,5},{5,4},{6,7},{7,6},{8,9},{9,8},{10,11... | collective-permute-start | bytes 1179656 | tf_op jit(solution)/shard_map/ppermute | solution.py:287
  251.5 12.1 %collective-permute-start.2 = (f32[16,48,1,128]{3,1,0,2:T(8,128)S(1)}, f32[16,48,1,128]{3,1,0,2:T(8,128)S(1)}, u32[]{:S(2)}, u32[]{:S(2)}) collective-permute-start(f32[16,48,1,128]{3,1,0,2:T(8,128)S(1)} %add.46), channel_id=1, source_target_pairs={{0,1},{1,0},{2,3},{3,2},{4,5},{5,4},{6,7},{7,6},{8,9},{9,8},{10,11... | collective-permute-start | bytes 1179656 | tf_op jit(solution)/shard_map/ppermute | solution.py:287
  259.3 7.8 %collective-permute-start.5 = (f32[16,48,1,128]{3,1,0,2:T(8,128)S(1)}, f32[16,48,1,128]{3,1,0,2:T(8,128)S(1)}, u32[]{:S(2)}, u32[]{:S(2)}) collective-permute-start(f32[16,48,1,128]{3,1,0,2:T(8,128)S(1)} %add.49), channel_id=1, source_target_pairs={{0,2},{1,3},{2,0},{3,1},{4,6},{5,7},{6,4},{7,5},{8,10},{9,11},{10,... | collective-permute-start | bytes 1179656 | tf_op jit(solution)/shard_map/ppermute | solution.py:287
